TPU v7x, 32 devices: a whole 2x2x4 slice. The times are simulated.
32 devices in a mesh: gx: 8 (over y, x, core), gy: 4 (over z).
Axes of the slice: x: 2, y: 2, z: 4, core: 2. Of those that a mesh axis runs over, the one named last changes fastest.
Arguments:
- u_old: float32 [3, 256, 128, 256], P(None, 'gx', 'gy'), may hold values from -0.6 to 0.6
- density: float32 [256, 128, 256], P('gx', 'gy'), may hold values from 0.5 to 2
- offsets: float32 [3, 512, 128], P(None, ('gx', 'gy')), may hold values from 0 to 1
- forces: float32 [3, 512, 128], P(None, ('gx', 'gy')), may hold values from -60 to 60
- base_x: int32 [512, 128], P(('gx', 'gy')), may hold values from 0 to 31
- base_y: int32 [512, 128], P(('gx', 'gy')), may hold values from 0 to 31
- base_z: int32 [512, 128], P(('gx', 'gy')), may hold values from 0 to 255
- tile_count: int32 [32], P(('gx', 'gy')), may hold values from 1 to 16, as said below
Outputs:
- u_new: float32 [3, 256, 128, 256], P(None, 'gx', 'gy')
- marker_velocity: float32 [3, 512, 128], P(None, ('gx', 'gy'))
Inputs may be any that keep to these rules, and one draw needn't show every extreme that they name: `tile_count`: every draw has a device with exactly 16 live tiles; loads are skewed, with a mean near a quarter of that.
All inputs are finite; a program needn't handle non-finite values.
Results may differ from a plain program's by a relative error of at most 0.000075.
Values sent between devices are 32-bit elements; how exact they have to be, the bound alone decides.
A program may use at most 64 MiB of HBM per device.

v0:
```python
import jax
import jax.numpy as jnp
from jax import lax
from jax.sharding import PartitionSpec as P


def shifted(value, axis, steps):
    count = lax.axis_size(axis)
    pairs = [(source, (source + steps) % count) for source in range(count)]
    return lax.ppermute(value, axis, pairs)


def with_halo(cells, sides, width):
    for axis, dim in sides:
        count = lax.axis_size(axis)
        head = lax.slice_in_dim(cells, 0, width, axis=dim)
        tail = lax.slice_in_dim(cells, cells.shape[dim] - width, cells.shape[dim], axis=dim)
        cells = jnp.concatenate(
            [
                lax.ppermute(tail, axis, [(i, (i + 1) % count) for i in range(count)]),
                cells,
                lax.ppermute(head, axis, [((i + 1) % count, i) for i in range(count)]),
            ],
            axis=dim,
        )
    return cells


def stencil(frac):
    root = jnp.sqrt(1.0 + 4.0 * frac - 4.0 * frac * frac)
    return [
        (3.0 - 2.0 * frac - root) / 8.0,
        (3.0 - 2.0 * frac + root) / 8.0,
        (1.0 + 2.0 * frac + root) / 8.0,
        (1.0 + 2.0 * frac - root) / 8.0,
    ]


def axis_weights(frac, base_cell, length, periodic):
    four = stencil(frac)
    column = lax.broadcasted_iota(jnp.int32, (base_cell.shape[0], length), 1)
    total = jnp.zeros((base_cell.shape[0], length), jnp.float32)
    for shift_a in range(4):
        if periodic:
            target = (base_cell + shift_a - 1) % length
        else:
            target = base_cell + shift_a + 1
        total = total + jnp.where(column == target[:, None], four[shift_a][:, None], 0.0)
    return total


def block_weights(offsets, base_x, base_y, base_z, start, block, outer_x, outer_y, depth_z):
    offset_part = lax.dynamic_slice_in_dim(offsets, start, block, 1).reshape(3, -1)
    cells_x = lax.dynamic_slice_in_dim(base_x, start, block, 0).reshape(-1)
    cells_y = lax.dynamic_slice_in_dim(base_y, start, block, 0).reshape(-1)
    cells_z = lax.dynamic_slice_in_dim(base_z, start, block, 0).reshape(-1)
    along_x = axis_weights(offset_part[0], cells_x, outer_x, False)
    along_y = axis_weights(offset_part[1], cells_y, outer_y, False)
    along_z = axis_weights(offset_part[2], cells_z, depth_z, True)
    plane = (along_x[:, :, None] * along_y[:, None, :]).reshape(cells_x.shape[0], outer_x * outer_y)
    return (plane, along_z)


def fold_x(grid, inner, depth):
    upper = shifted(grid[:, inner + 4 - depth : inner + 4], "gx", 1)
    lower = shifted(grid[:, 0:depth], "gx", -1)
    grid = grid.at[:, 4 - depth : 4].add(upper)
    return grid.at[:, inner : inner + depth].add(lower)


def fold_y(grid, inner, depth):
    upper = shifted(grid[:, :, inner + 4 - depth : inner + 4], "gy", 1)
    lower = shifted(grid[:, :, 0:depth], "gy", -1)
    grid = grid.at[:, :, 4 - depth : 4].add(upper)
    return grid.at[:, :, inner : inner + depth].add(lower)


def on_device(u_old, density, offsets, forces, base_x, base_y, base_z, tile_count):
    time_step = 0.5
    _, size_x, size_y, depth_z = u_old.shape
    slots, width = base_x.shape
    outer_x, outer_y = (size_x + 4, size_y + 4)
    plane_cells = outer_x * outer_y
    state = jnp.concatenate([u_old, density[None]], axis=0)
    state_pad = with_halo(state, (("gx", 1), ("gy", 2)), 2)
    count = tile_count[0]
    live = (lax.broadcasted_iota(jnp.int32, (slots, width), 0) < count).astype(jnp.float32)
    load = forces * live[None]
    block = min(8, slots)
    markers = block * width
    turns = slots // block

    def spread_block(turn, grid):
        start = turn * block
        plane, along_z = block_weights(
            offsets, base_x, base_y, base_z, start, block, outer_x, outer_y, depth_z
        )
        load_part = lax.dynamic_slice_in_dim(load, start, block, 1).reshape(3, markers)
        heavy = (along_z[:, None, :] * load_part.T[:, :, None]).reshape(markers, 3 * depth_z)
        return grid + lax.dot_general(
            plane,
            heavy,
            (((0,), (0,)), ((), ())),
            precision=lax.Precision.HIGHEST,
            preferred_element_type=jnp.float32,
        )

    flat_grid = lax.fori_loop(
        0, turns, spread_block, jnp.zeros((plane_cells, 3 * depth_z), jnp.float32)
    )
    grid = flat_grid.reshape(outer_x, outer_y, 3, depth_z).transpose(2, 0, 1, 3)
    grid = fold_y(fold_x(grid, size_x, 4), size_y, 4)
    u_pad = state_pad[:3] + time_step * grid / state_pad[3][None]
    u_new = u_pad[:, 2 : size_x + 2, 2 : size_y + 2]
    table = (
        u_pad.reshape(3, plane_cells, depth_z).transpose(1, 0, 2).reshape(plane_cells, 3 * depth_z)
    )

    def read_block(turn, velocity):
        start = turn * block
        plane, along_z = block_weights(
            offsets, base_x, base_y, base_z, start, block, outer_x, outer_y, depth_z
        )
        picked = jnp.dot(
            plane, table, precision=lax.Precision.HIGHEST, preferred_element_type=jnp.float32
        ).reshape(markers, 3, depth_z)
        values = jnp.sum(picked * along_z[:, None, :], axis=2).T.reshape(3, block, width)
        return lax.dynamic_update_slice_in_dim(velocity, values, start, 1)

    velocity = lax.fori_loop(0, turns, read_block, jnp.zeros((3, slots, width), jnp.float32))
    return (u_new, velocity * live[None])


def solution(mesh):
    in_specs = (
        P(None, "gx", "gy", None),
        P("gx", "gy", None),
        P(None, ("gx", "gy"), None),
        P(None, ("gx", "gy"), None),
        P(("gx", "gy"), None),
        P(("gx", "gy"), None),
        P(("gx", "gy"), None),
        P(("gx", "gy")),
    )
    out_specs = (P(None, "gx", "gy", None), P(None, ("gx", "gy"), None))
    return jax.shard_map(
        on_device, mesh=mesh, in_specs=in_specs, out_specs=out_specs, check_vma=False
    )
```

profile of v0, /device:TPU:0, one launch (start us, length us, event | category | flops | bytes accessed | tf_op | source)
XLA Modules:
  0.0 207.2 jit_solution(9592910399393990929)
XLA Ops:
  2.1 56.9 %while.42 = (s32[]{:T(128)}, f32[1296,768]{1,0:T(8,128)}, s32[16,128]{1,0:T(8,128)}, f32[3,16,128]{2,1,0:T(8,128)}, s32[16,128]{1,0:T(8,128)}, /*index=5*/s32[16...) while((s32[]{:T(128)}, f32[1296,768]{1,0:T(8,128)}, ...), condition=%wide.region_1.2_spmd.clone, body=%wide.region_0.1_spmd.clone.sunk | while | flops 12238491648 | bytes 38490368 | solution.py:108
  3.7 3.3 %broadcast_multiply_fusion.9 = f32[1024,36,36]{0,2,1:T(8,128)} fusion(f32[1024,36]{0,1:T(8,128)S(1)} %select_add_fusion.17, f32[1024,36]{0,1:T(8,128)S(1)} %select_add_fusion.18), kind=kLoop, calls=%fused_computation.74.clone.1 | loop fusion | flops 1327104 | bytes 5603328 | tf_op jit(solution)/shard_map/while/body/eval_jaxpr/mul | solution.py:60
  7.0 6.4 %mul.1293 = f32[1024,1296]{0,1:T(8,128)} reshape(f32[1024,36,36]{0,2,1:T(8,128)} %broadcast_multiply_fusion.9) | data formatting | bytes 10616832 | tf_op jit(solution)/shard_map/while/body/eval_jaxpr/mul | solution.py:60
  14.2 16.2 %select_add_fusion.20 = f32[1296,768]{1,0:T(8,128)} fusion(f32[1296,768]{1,0:T(8,128)} %get-tuple-element.920, f32[1024,1296]{0,1:T(8,128)} %mul.1293, f32[1024,768]{0,1:T(8,128)S(1)} %bitcast.226, pred[]{:T(512)S(6)} %compare.65), kind=kOutput, calls=%fused_computation.73.clone.1 | convolution fusion | flops 12232581120 | bytes 16416769 | tf_op jit(solution)/shard_map/while/body/eval_jaxpr/dot_general | solution.py:100
  32.0 3.3 %broadcast_multiply_fusion.9 = f32[1024,36,36]{0,2,1:T(8,128)} fusion(f32[1024,36]{0,1:T(8,128)S(1)} %select_add_fusion.17, f32[1024,36]{0,1:T(8,128)S(1)} %select_add_fusion.18), kind=kLoop, calls=%fused_computation.74.clone.1 | loop fusion | flops 1327104 | bytes 5603328 | tf_op jit(solution)/shard_map/while/body/eval_jaxpr/mul | solution.py:60
  35.3 6.4 %mul.1293 = f32[1024,1296]{0,1:T(8,128)} reshape(f32[1024,36,36]{0,2,1:T(8,128)} %broadcast_multiply_fusion.9) | data formatting | bytes 10616832 | tf_op jit(solution)/shard_map/while/body/eval_jaxpr/mul | solution.py:60
  42.4 16.6 %select_add_fusion.20 = f32[1296,768]{1,0:T(8,128)} fusion(f32[1296,768]{1,0:T(8,128)} %get-tuple-element.920, f32[1024,1296]{0,1:T(8,128)} %mul.1293, f32[1024,768]{0,1:T(8,128)S(1)} %bitcast.226, pred[]{:T(512)S(6)} %compare.65), kind=kOutput, calls=%fused_computation.73.clone.1 | convolution fusion | flops 12232581120 | bytes 16416769 | tf_op jit(solution)/shard_map/while/body/eval_jaxpr/dot_general | solution.py:100
  59.0 7.5 %reshape.2005 = f32[36,36,3,256]{3,2,1,0:T(4,128)} reshape(f32[1296,768]{1,0:T(8,128)} %get-tuple-element.602) | data formatting | bytes 7962624 | tf_op jit(solution)/shard_map/reshape | solution.py:111
  83.2 2.6 %collective-permute-start.1 = (f32[4,2,32,256]{3,0,2,1:T(4,128)S(1)}, f32[4,2,32,256]{3,0,2,1:T(4,128)S(1)}, u32[]{:S(2)}, u32[]{:S(2)}) collective-permute-start(f32[4,2,32,256]{3,0,2,1:T(4,128)S(1)} %get-tuple-element.723), channel_id=1, source_target_pairs={{4,0},{8,4},{12,8},{16,12},{20,16},{24,20},{28,24},{0,28},{5,1},{9... | collective-permute-start | bytes 786440 | tf_op jit(solution)/shard_map/ppermute | solution.py:22
  85.8 6.9 %collective-permute-done = f32[4,2,32,256]{3,0,2,1:T(4,128)S(1)} collective-permute-done((f32[4,2,32,256]{3,0,2,1:T(4,128)S(1)}, f32[4,2,32,256]{3,0,2,1:T(4,128)S(1)}, u32[]{:S(2)}, u32[]{:S(2)}) %collective-permute-start) | collective-permute-done | bytes 262176 | tf_op jit(solution)/shard_map/ppermute | solution.py:20
  103.3 4.3 %collective-permute-done.2 = f32[4,36,2,256]{3,0,2,1:T(4,128)S(1)} collective-permute-done((f32[4,36,2,256]{3,0,2,1:T(4,128)}, f32[4,36,2,256]{3,0,2,1:T(4,128)S(1)}, u32[]{:S(2)}, u32[]{:S(2)}) %collective-permute-start.2) | collective-permute-done | bytes 294944 | tf_op jit(solution)/shard_map/ppermute | solution.py:20
  107.6 5.8 %collective-permute-done.3 = f32[4,36,2,256]{3,0,2,1:T(4,128)S(1)} collective-permute-done((f32[4,36,2,256]{3,0,2,1:T(4,128)S(1)}, f32[4,36,2,256]{3,0,2,1:T(4,128)S(1)}, u32[]{:S(2)}, u32[]{:S(2)}) %collective-permute-start.3) | collective-permute-done | bytes 294944 | tf_op jit(solution)/shard_map/ppermute | solution.py:22
  113.4 8.1 %pad_maximum_fusion.1 = f32[1,36,36,256]{3,0,2,1:T(1,128)S(1)} fusion(f32[4,36,2,256]{3,0,2,1:T(4,128)S(1)} %collective-permute-done.3, f32[4,36,2,256]{3,0,2,1:T(4,128)S(1)} %collective-permute-done.2, f32[4,2,32,256]{3,0,2,1:T(4,128)S(1)} %collective-permute-done.1, f32[4,2,32,256]{3,0,2,1:T(4,128)S(1)} %collective-permute-done, ...), kind=kLoop, calls=%fused_computation.151 | loop fusion | flops 1658880 | bytes 6635520 | tf_op jit(solution)/shard_map/slice | solution.py:113
  126.5 4.5 %pad_maximum_fusion = f32[4,36,36,256]{3,0,2,1:T(4,128)S(1)} fusion(f32[4,36,2,256]{3,0,2,1:T(4,128)S(1)} %collective-permute-done.3, f32[4,2,32,256]{3,0,2,1:T(4,128)S(1)} %collective-permute-done.1, f32[1,32,32,256]{3,0,2,1:T(1,128)S(1)} %broadcast_in_dim.488, f32[3,32,32,256]{3,0,2,1:T(4,128)S(1)} %copy-done.1, ...), kind=kLoop, calls=%fused_computation.149 | loop fusion | flops 6635520 | bytes 10616832 | tf_op jit(solution)/shard_map/concatenate | solution.py:18
  131.0 5.6 %collective-permute-done.7 = f32[3,36,4,256]{3,2,1,0:T(4,128)S(1)} collective-permute-done((f32[3,36,4,256]{3,2,1,0:T(4,128)S(1)}, f32[3,36,4,256]{3,2,1,0:T(4,128)S(1)}, u32[]{:S(2)}, u32[]{:S(2)}) %collective-permute-start.7) | collective-permute-done | bytes 442400 | tf_op jit(solution)/shard_map/ppermute | solution.py:10
  140.2 2.7 %copy.27 = f32[3,32,32,256]{3,2,1,0:T(8,128)} copy(f32[3,32,32,256]{3,0,2,1:T(4,128)S(1)} %slice.262) | data formatting | bytes 6291456
  142.9 6.5 %copy.26 = f32[3,1296,256]{1,2,0:T(8,128)} copy(f32[3,1296,256]{2,0,1:T(4,128)} %bitcast.227) | data formatting | bytes 7962624 | tf_op jit(solution)/shard_map/reshape | solution.py:116
  149.5 57.1 %while.41 = (s32[]{:T(128)}, f32[3,16,128]{2,1,0:T(8,128)S(1)}, s32[16,128]{1,0:T(8,128)S(1)}, f32[3,16,128]{2,1,0:T(8,128)S(1)}, s32[16,128]{1,0:T(8,128)S(1)},...) while((s32[]{:T(128)}, f32[3,16,128]{2,1,0:T(8,128)S(1)}, ...), condition=%wide.region_4.5_spmd, body=%wide.region_2.4_spmd.sunk | while | flops 12237284352 | bytes 28164316 | solution.py:130
  149.7 3.3 %broadcast_multiply_fusion.8 = f32[1024,36,36]{0,2,1:T(8,128)} fusion(f32[1024,36]{0,1:T(8,128)S(1)} %select_add_fusion.14, f32[1024,36]{0,1:T(8,128)S(1)} %select_add_fusion.15), kind=kLoop, calls=%fused_computation.1.clone.1 | loop fusion | flops 1327104 | bytes 5603328 | tf_op jit(solution)/shard_map/while/body/eval_jaxpr/mul | solution.py:60
  153.0 6.4 %reshape.2014 = f32[1024,1296,1]{0,1,2:T(8,128)} reshape(f32[1024,36,36]{0,2,1:T(8,128)} %broadcast_multiply_fusion.8) | data formatting | bytes 10616832 | tf_op jit(solution)/shard_map/while/body/eval_jaxpr/mul | solution.py:60
  159.7 18.3 %multiply_reduce_fusion.2 = f32[1024,3]{0,1:T(4,128)S(1)} fusion(f32[1024,1296,1]{0,1,2:T(8,128)} %reshape.2014, f32[3,256,1296]{2,1,0:T(8,128)} %bitcast.232, f32[1024,256]{0,1:T(8,128)S(1)} %select_add_fusion.16), kind=kOutput, calls=%fused_computation.clone.1 | convolution fusion | flops 12232160256 | bytes 10350592 | tf_op jit(solution)/shard_map/while/body/eval_jaxpr/dot_general | solution.py:124
  178.2 3.3 %broadcast_multiply_fusion.8 = f32[1024,36,36]{0,2,1:T(8,128)} fusion(f32[1024,36]{0,1:T(8,128)S(1)} %select_add_fusion.14, f32[1024,36]{0,1:T(8,128)S(1)} %select_add_fusion.15), kind=kLoop, calls=%fused_computation.1.clone.1 | loop fusion | flops 1327104 | bytes 5603328 | tf_op jit(solution)/shard_map/while/body/eval_jaxpr/mul | solution.py:60
  181.5 6.4 %reshape.2014 = f32[1024,1296,1]{0,1,2:T(8,128)} reshape(f32[1024,36,36]{0,2,1:T(8,128)} %broadcast_multiply_fusion.8) | data formatting | bytes 10616832 | tf_op jit(solution)/shard_map/while/body/eval_jaxpr/mul | solution.py:60
  188.3 18.3 %multiply_reduce_fusion.2 = f32[1024,3]{0,1:T(4,128)S(1)} fusion(f32[1024,1296,1]{0,1,2:T(8,128)} %reshape.2014, f32[3,256,1296]{2,1,0:T(8,128)} %bitcast.232, f32[1024,256]{0,1:T(8,128)S(1)} %select_add_fusion.16), kind=kOutput, calls=%fused_computation.clone.1 | convolution fusion | flops 12232160256 | bytes 10350592 | tf_op jit(solution)/shard_map/while/body/eval_jaxpr/dot_general | solution.py:124
  (93 shorter events, 43.1 us)
Async XLA Ops:
  7.0 6.4 %copy-start.8 = (s32[16,128]{1,0:T(8,128)S(1)}, s32[16,128]{1,0:T(8,128)}, u32[]{:S(2)}) copy-start(s32[16,128]{1,0:T(8,128)} %get-tuple-element.937) | copy-start | bytes 24580 | tf_op jit(solution)/shard_map/while
  35.3 6.4 %copy-start.8 = (s32[16,128]{1,0:T(8,128)S(1)}, s32[16,128]{1,0:T(8,128)}, u32[]{:S(2)}) copy-start(s32[16,128]{1,0:T(8,128)} %get-tuple-element.937) | copy-start | bytes 24580 | tf_op jit(solution)/shard_map/while
  59.0 14.1 %copy-start.4 = (f32[3,32,32,256]{3,2,1,0:T(8,128)S(1)}, f32[3,32,32,256]{3,2,1,0:T(8,128)}, u32[]{:S(2)}) copy-start(f32[3,32,32,256]{3,2,1,0:T(8,128)} %param.20) | copy-start | bytes 9437188
  68.8 9.7 %collective-permute-start.4 = (f32[3,4,36,256]{3,1,2,0:T(4,128)}, f32[3,4,36,256]{3,1,2,0:T(4,128)}, u32[]{:S(2)}, u32[]{:S(2)}) collective-permute-start(f32[3,4,36,256]{3,1,2,0:T(4,128)} %copy.18), channel_id=1, source_target_pairs={{0,4},{4,8},{8,12},{12,16},{16,20},{20,24},{24,28},{28,0},{1,5},{5... | collective-permute-start | bytes 1327112 | tf_op jit(solution)/shard_map/ppermute | solution.py:10
  73.1 2.6 %copy-start.6 = (f32[32,32,256]{2,1,0:T(8,128)S(1)}, f32[32,32,256]{2,1,0:T(8,128)}, u32[]{:S(2)}) copy-start(f32[32,32,256]{2,1,0:T(8,128)} %param.21) | copy-start | bytes 3145732
  73.1 5.3 %copy-start.5 = (f32[4,36,3,256]{3,2,1,0:T(4,128)S(1)}, f32[4,36,3,256]{3,2,1,0:T(4,128)}, u32[]{:S(2)}) copy-start(f32[4,36,3,256]{3,2,1,0:T(4,128)} %reshape.2006) | copy-start | bytes 1327108
  75.7 18.6 %copy-start = (f32[3,32,32,256]{3,0,2,1:T(4,128)}, f32[3,32,32,256]{3,0,2,1:T(4,128)S(1)}, u32[]{:S(2)}) copy-start(f32[3,32,32,256]{3,0,2,1:T(4,128)S(1)} %copy.17) | copy-start | bytes 9437188
  81.2 18.5 %collective-permute-start.5 = (f32[3,4,36,256]{3,1,2,0:T(4,128)S(1)}, f32[3,4,36,256]{3,1,2,0:T(4,128)S(1)}, u32[]{:S(2)}, u32[]{:S(2)}) collective-permute-start(f32[3,4,36,256]{3,1,2,0:T(4,128)S(1)} %copy.20), channel_id=1, source_target_pairs={{0,28},{4,0},{8,4},{12,8},{16,12},{20,16},{24,20},{28,24},{1,29},{... | collective-permute-start | bytes 1327112 | tf_op jit(solution)/shard_map/ppermute | solution.py:10
  83.1 9.6 %collective-permute-start = (f32[4,2,32,256]{3,0,2,1:T(4,128)S(1)}, f32[4,2,32,256]{3,0,2,1:T(4,128)S(1)}, u32[]{:S(2)}, u32[]{:S(2)}) collective-permute-start(f32[4,2,32,256]{3,0,2,1:T(4,128)S(1)} %get-tuple-element.722), channel_id=1, source_target_pairs={{0,4},{4,8},{8,12},{12,16},{16,20},{20,24},{24,28},{28,0},{1,5},{5... | collective-permute-start | bytes 786440 | tf_op jit(solution)/shard_map/ppermute | solution.py:20
  83.2 11.1 %collective-permute-start.1 = (f32[4,2,32,256]{3,0,2,1:T(4,128)S(1)}, f32[4,2,32,256]{3,0,2,1:T(4,128)S(1)}, u32[]{:S(2)}, u32[]{:S(2)}) collective-permute-start(f32[4,2,32,256]{3,0,2,1:T(4,128)S(1)} %get-tuple-element.723), channel_id=1, source_target_pairs={{4,0},{8,4},{12,8},{16,12},{20,16},{24,20},{28,24},{0,28},{5,1},{9... | collective-permute-start | bytes 786440 | tf_op jit(solution)/shard_map/ppermute | solution.py:22
  95.3 12.3 %collective-permute-start.2 = (f32[4,36,2,256]{3,0,2,1:T(4,128)}, f32[4,36,2,256]{3,0,2,1:T(4,128)S(1)}, u32[]{:S(2)}, u32[]{:S(2)}) collective-permute-start(f32[4,36,2,256]{3,0,2,1:T(4,128)} %get-tuple-element.716), channel_id=1, source_target_pairs={{0,1},{1,2},{2,3},{3,0},{4,5},{5,6},{6,7},{7,4},{8,9},{9,10},{10,1... | collective-permute-start | bytes 884744 | tf_op jit(solution)/shard_map/ppermute | solution.py:20
  97.6 15.8 %collective-permute-start.3 = (f32[4,36,2,256]{3,0,2,1:T(4,128)S(1)}, f32[4,36,2,256]{3,0,2,1:T(4,128)S(1)}, u32[]{:S(2)}, u32[]{:S(2)}) collective-permute-start(f32[4,36,2,256]{3,0,2,1:T(4,128)S(1)} %get-tuple-element.717), channel_id=1, source_target_pairs={{1,0},{2,1},{3,2},{0,3},{5,4},{6,5},{7,6},{4,7},{9,8},{10,9},{11,1... | collective-permute-start | bytes 884744 | tf_op jit(solution)/shard_map/ppermute | solution.py:22
  103.2 20.2 %copy-start.3 = (f32[3,36,36,256]{3,0,2,1:T(4,128)S(1)}, f32[3,36,36,256]{3,0,2,1:T(4,128)}, u32[]{:S(2)}) copy-start(f32[3,36,36,256]{3,0,2,1:T(4,128)} %fusion.23) | copy-start | bytes 11943940
  103.2 23.2 %copy-start.1 = (f32[3,32,32,256]{3,0,2,1:T(4,128)S(1)}, f32[3,32,32,256]{3,0,2,1:T(4,128)}, u32[]{:S(2)}) copy-start(f32[3,32,32,256]{3,0,2,1:T(4,128)} %copy-done) | copy-start | bytes 9437188
  103.2 20.1 %collective-permute-start.6 = (f32[3,36,4,256]{3,2,1,0:T(4,128)S(1)}, f32[3,36,4,256]{3,2,1,0:T(4,128)S(1)}, u32[]{:S(2)}, u32[]{:S(2)}) collective-permute-start(f32[3,36,4,256]{3,2,1,0:T(4,128)S(1)} %copy.22), channel_id=1, source_target_pairs={{0,1},{1,2},{2,3},{3,0},{4,5},{5,6},{6,7},{7,4},{8,9},{9,10},{10,1... | collective-permute-start | bytes 1327112 | tf_op jit(solution)/shard_map/ppermute | solution.py:10
  124.1 12.5 %collective-permute-start.7 = (f32[3,36,4,256]{3,2,1,0:T(4,128)S(1)}, f32[3,36,4,256]{3,2,1,0:T(4,128)S(1)}, u32[]{:S(2)}, u32[]{:S(2)}) collective-permute-start(f32[3,36,4,256]{3,2,1,0:T(4,128)S(1)} %copy.24), channel_id=1, source_target_pairs={{0,3},{1,0},{2,1},{3,2},{4,7},{5,4},{6,5},{7,6},{8,11},{9,8},{10,9... | collective-permute-start | bytes 1327112 | tf_op jit(solution)/shard_map/ppermute | solution.py:10
  139.5 3.4 %copy-start.2 = (f32[3,36,36,256]{3,0,2,1:T(4,128)}, f32[3,36,36,256]{3,0,2,1:T(4,128)S(1)}, u32[]{:S(2)}) copy-start(f32[3,36,36,256]{3,0,2,1:T(4,128)S(1)} %divide_add_fusion) | copy-start | bytes 11943940
  142.9 6.5 %copy-start.7 = (f32[3,16,128]{2,1,0:T(8,128)S(1)}, f32[3,16,128]{2,1,0:T(8,128)}, u32[]{:S(2)}) copy-start(f32[3,16,128]{2,1,0:T(8,128)} %get-tuple-element.988) | copy-start | bytes 73732
  142.9 6.5 %copy-start.9 = (s32[16,128]{1,0:T(8,128)S(1)}, s32[16,128]{1,0:T(8,128)}, u32[]{:S(2)}) copy-start(s32[16,128]{1,0:T(8,128)} %get-tuple-element.998) | copy-start | bytes 24580
  142.9 6.5 %copy-start.10 = (s32[16,128]{1,0:T(8,128)S(1)}, s32[16,128]{1,0:T(8,128)}, u32[]{:S(2)}) copy-start(s32[16,128]{1,0:T(8,128)} %get-tuple-element.999) | copy-start | bytes 24580
  142.9 6.6 %copy-start.11 = (s32[16,128]{1,0:T(8,128)S(1)}, s32[16,128]{1,0:T(8,128)}, u32[]{:S(2)}) copy-start(s32[16,128]{1,0:T(8,128)} %get-tuple-element.1000) | copy-start | bytes 24580
where the time goes:
time: 209 us; the launch traced here: 207 us
  matrix products  69.3 us (33%)
  local copies, waits for them, and re-layouts  54.2 us (26%)
  other arithmetic  42.5 us (20%)
  waiting for transfers between devices  27.9 us (13%)
  starting transfers between devices  11.6 us (6%)
    dot_general x2, matrix products, read_block(): jnp.dot(plane, table, precision=lax.Precision.HIGHEST, preferred_element_...  36.5 us
    dot_general x2, matrix products, spread_block(): lax.dot_general(plane, heavy, (((0,), (0,)), ((), ())), precision=lax.Pre...  32.8 us
    mul x4, local copies, waits for them, and re-layouts, block_weights(): along_x[:, :, None] * along_y[:, None, :]  25.4 us
    mul x4, other arithmetic, block_weights(): along_x[:, :, None] * along_y[:, None, :]  13.1 us
    ppermute x2, waiting for transfers between devices, with_halo(): lax.ppermute(tail, axis, [(i, (i + 1) % count) for i in range(count)])  11.2 us
    ppermute x4, waiting for transfers between devices, shifted(): return lax.ppermute(value, axis, pairs)  9.26 us
    slice x1, other arithmetic, on_device(): u_pad = state_pad[:3] + time_step * grid / state_pad[3][None]  8.11 us
    reshape x1, local copies, waits for them, and re-layouts, on_device(): grid = flat_grid.reshape(outer_x, outer_y, 3, depth_z).transpose(2, 0, 1, 3)  7.49 us
  transfers between devices with their start and end apart: 8, of which 7 were waited for; matrix products, arithmetic and copies ran while one was open for 12% of the time, Pallas kernels for 0%

commit v1 on v0

v1 whole, which is shorter than its diff:
```python
import functools

import jax
import jax.numpy as jnp
from jax import lax
from jax.experimental import pallas as pl
from jax.experimental.pallas import tpu as pltpu
from jax.sharding import PartitionSpec as P

VMEM_LIMIT = 60 * 1024 * 1024


def divisor(count, most):
    return max(d for d in range(1, most + 1) if count % d == 0)


def moved(value, step_x, step_y):
    if step_y == 0:
        n = lax.axis_size("gx")
        return lax.ppermute(value, "gx", [(i, (i + step_x) % n) for i in range(n)])
    if step_x == 0:
        n = lax.axis_size("gy")
        return lax.ppermute(value, "gy", [(i, (i + step_y) % n) for i in range(n)])
    nx, ny = lax.axis_size("gx"), lax.axis_size("gy")
    pairs = [
        (i * ny + j, ((i + step_x) % nx) * ny + (j + step_y) % ny)
        for i in range(nx)
        for j in range(ny)
    ]
    return lax.ppermute(value, ("gx", "gy"), pairs)


def stencil(frac):
    root = jnp.sqrt(1.0 + 4.0 * frac - 4.0 * frac * frac)
    return [
        (3.0 - 2.0 * frac - root) / 8.0,
        (3.0 - 2.0 * frac + root) / 8.0,
        (1.0 + 2.0 * frac + root) / 8.0,
        (1.0 + 2.0 * frac - root) / 8.0,
    ]


def pick(delta, four):
    total = jnp.where(delta == 0, four[0], 0.0)
    for k in range(1, 4):
        total = jnp.where(delta == k, four[k], total)
    return total


def wrapped(delta, length):
    delta = jnp.where(delta < 0, delta + length, delta)
    return jnp.where(delta >= length, delta - length, delta)


def edge_weights(frac, base, rows, size):
    row = lax.broadcasted_iota(jnp.int32, (rows, base.shape[1]), 0)
    cell = jnp.where(row == size + 2, -1, row)
    cell = jnp.where(row > size + 2, -8, cell)
    return pick(cell - base + 1, stencil(frac))


def halves(value):
    high = value.astype(jnp.bfloat16)
    low = (value - high.astype(jnp.float32)).astype(jnp.bfloat16)
    return high, low


def edges(size):
    return (size - 1, size, size + 1), (size + 2, 0, 1)


def spread_kernel(size_x, size_y, feat, base, grid, *refs):
    slabs, (wx_s, wy_s, high_s, low_s) = refs[:8], refs[8:]
    planes, rows, depth = grid.shape[1], grid.shape[2], grid.shape[3]
    markers = feat.shape[1]
    wx_s[...] = edge_weights(feat[0:1, :], base[0:1, :], wx_s.shape[0], size_x)
    wy_s[...] = edge_weights(feat[1:2, :], base[1:2, :], rows, size_y)
    four = stencil(feat[2:3, :])
    column = jnp.concatenate(
        four + [base[2:3, :].astype(jnp.float32)] + [feat[3 + c : 4 + c, :] for c in range(3)], axis=0
    ).T
    cut = 256 if markers % 256 == 0 else 128
    for start in range(0, markers, cut):
        part = column[start : start + cut]
        lane = lax.broadcasted_iota(jnp.int32, (cut, depth), 1)
        delta = wrapped(lane - part[:, 4:5].astype(jnp.int32) + 1, depth)
        wz = pick(delta, [part[:, k : k + 1] for k in range(4)])
        for c in range(3):
            high, low = halves(wz * part[:, 5 + c : 6 + c])
            high_s[start : start + cut, c * depth : (c + 1) * depth] = high
            low_s[start : start + cut, c * depth : (c + 1) * depth] = low
    group = divisor(planes, 8)

    def turn(g, carry):
        first = g * group
        left = jnp.concatenate(
            [wy_s[...] * wx_s[pl.ds(first + j, 1), :] for j in range(group)], axis=0
        )
        high, low = halves(left)
        dot = functools.partial(jnp.dot, preferred_element_type=jnp.float32)
        total = dot(high, high_s[...]) + dot(low, high_s[...]) + dot(high, low_s[...])
        for j in range(group):
            for c in range(3):
                grid[c, first + j] = total[j * rows : (j + 1) * rows, c * depth : (c + 1) * depth]
        return carry

    lax.fori_loop(0, planes // group, turn, 0)
    sides_x, sides_y = edges(size_x), edges(size_y)
    for side in range(2):
        for c in range(3):
            for j, p in enumerate(sides_x[side]):
                slabs[side][c, j] = grid[c, p]
                for other in range(2):
                    for i, r in enumerate(sides_y[other]):
                        slabs[4 + 2 * side + other][c, j, i : i + 1] = grid[c, p, r : r + 1]
            for i, r in enumerate(sides_y[side]):
                for p in range(planes):
                    slabs[2 + side][c, i, p : p + 1] = grid[c, p, r : r + 1]


def read_kernel(size_x, size_y, time_step, *refs):
    feat, base, grid, u_old, density, low_x, high_x, low_y, high_y = refs[:9]
    slabs, (u_new, velocity) = refs[9:17], refs[17:19]
    total, wx_s, wy_s, wz3, table = refs[19:]
    planes, rows, depth = grid.shape[1], grid.shape[2], grid.shape[3]
    markers = feat.shape[1]
    wx_s[...] = edge_weights(feat[0:1, :], base[0:1, :], wx_s.shape[0], size_x)
    wy_s[...] = edge_weights(feat[1:2, :], base[1:2, :], rows, size_y)
    cut = 256 if markers % 256 == 0 else 128
    for start in range(0, markers, cut):
        at = slice(start, start + cut)
        row = lax.broadcasted_iota(jnp.int32, (depth, cut), 0)
        delta = wrapped(row - base[2:3, at] + 1, depth)
        high, low = halves(pick(delta, stencil(feat[2:3, at])))
        wz3[0:depth, at] = high
        wz3[depth : 2 * depth, at] = high
        wz3[2 * depth :, at] = low
    total[...] = grid[...]
    near_x, near_y = edges(size_x)[::-1], edges(size_y)[::-1]
    for side in range(2):
        for c in range(3):
            for j, p in enumerate(near_x[side]):
                total[c, p] = total[c, p] + slabs[side][c, j]
                for other in range(2):
                    for i, r in enumerate(near_y[other]):
                        total[c, p, r : r + 1] = (
                            total[c, p, r : r + 1] + slabs[4 + 2 * side + other][c, j, i : i + 1]
                        )
            for i, r in enumerate(near_y[side]):
                for p in range(planes):
                    total[c, p, r : r + 1] = total[c, p, r : r + 1] + slabs[2 + side][c, i, p : p + 1]
    group = divisor(planes, 6)
    spare = jnp.ones((rows - size_y - 3, depth), jnp.float32)

    def plane_state(k, p):
        if p < size_x:
            main = density[p] if k == 3 else u_old[k, p]
        elif p < size_x + 2:
            main = high_x[k, p - size_x]
        else:
            main = low_x[k, 0]
        edge = [high_y[k, 0, p : p + 1], high_y[k, 1, p : p + 1], low_y[k, 0, p : p + 1], spare]
        return jnp.concatenate([main] + edge, axis=0)

    for g in range(planes // group):
        pieces = []
        for p in range(g * group, (g + 1) * group):
            scale = time_step / plane_state(3, p)
            for c in range(3):
                value = plane_state(c, p) + total[c, p] * scale
                if p < size_x:
                    u_new[c, p] = value[:size_y]
                pieces.append(value)
        high, low = halves(jnp.concatenate(pieces, axis=0))
        table[g, :, 0:depth] = high
        table[g, :, depth : 2 * depth] = low
        table[g, :, 2 * depth :] = high

    def turn(step, carry):
        at = pl.ds(pl.multiple_of(step * cut, cut), cut)
        right = wz3[:, at]
        wy = wy_s[:, at]
        sums = [jnp.zeros((8, cut), jnp.float32) for _ in range(3)]
        for g in range(planes // group):
            found = jnp.dot(table[g], right, preferred_element_type=jnp.float32)
            for j in range(group):
                p = g * group + j
                weight = wy * wx_s[p : p + 1, at]
                for c in range(3):
                    first = (j * 3 + c) * rows
                    product = found[first : first + rows] * weight
                    for r in range(0, rows, 8):
                        sums[c] = sums[c] + product[r : r + 8]
        velocity[:, at] = (
            jnp.concatenate([jnp.sum(s, axis=0, keepdims=True) for s in sums], axis=0) * feat[6:7, at]
        )
        return carry

    lax.fori_loop(0, markers // cut, turn, 0)


def on_device(u_old, density, offsets, forces, base_x, base_y, base_z, tile_count):
    time_step = 0.5
    _, size_x, size_y, depth = u_old.shape
    slots, width = base_x.shape
    markers = slots * width
    planes = size_x + 3
    rows = -(-(size_y + 3) // 8) * 8
    lines = -(-planes // 8) * 8
    f32, bf16 = jnp.float32, jnp.bfloat16
    live = (lax.broadcasted_iota(jnp.int32, (slots, width), 0) < tile_count[0]).astype(f32)
    feat = jnp.concatenate([offsets, forces * live[None], live[None]], axis=0).reshape(7, markers)
    base = jnp.stack([base_x, base_y, base_z], axis=0).reshape(3, markers)

    up = jnp.concatenate([u_old[:, size_x - 1 :], density[None, size_x - 1 :]], axis=0)
    down = jnp.concatenate([u_old[:, :2], density[None, :2]], axis=0)
    low_x, high_x = moved(up, 1, 0), moved(down, -1, 0)

    def strip(r):
        inner = jnp.concatenate([u_old[:, :, r], density[None, :, r]], axis=0)
        return jnp.concatenate([inner, high_x[:, :, r], low_x[:, :, r]], axis=1)

    low_y = moved(strip(size_y - 1)[:, None], 0, 1)
    high_y = moved(jnp.stack([strip(0), strip(1)], axis=1), 0, -1)

    params = pltpu.CompilerParams(vmem_limit_bytes=VMEM_LIMIT)
    slab_x = jax.ShapeDtypeStruct((3, 3, rows, depth), f32)
    slab_y = jax.ShapeDtypeStruct((3, 3, planes, depth), f32)
    corner = jax.ShapeDtypeStruct((3, 3, 3, depth), f32)
    whole = pl.BlockSpec(memory_space=pltpu.VMEM)
    flops = 6 * planes * rows * 3 * depth * markers
    cost = pl.CostEstimate(flops=flops, transcendentals=0, bytes_accessed=8 * planes * rows * depth)
    grid, *slabs = pl.pallas_call(
        functools.partial(spread_kernel, size_x, size_y),
        out_shape=[jax.ShapeDtypeStruct((3, planes, rows, depth), f32)]
        + [slab_x] * 2
        + [slab_y] * 2
        + [corner] * 4,
        in_specs=[whole] * 2,
        out_specs=[whole] * 9,
        scratch_shapes=[
            pltpu.VMEM((lines, markers), f32),
            pltpu.VMEM((rows, markers), f32),
            pltpu.VMEM((markers, 3 * depth), bf16),
            pltpu.VMEM((markers, 3 * depth), bf16),
        ],
        compiler_params=params,
        cost_estimate=cost,
        name="spread",
    )(feat, base)
    ways = [(1, 0), (-1, 0), (0, 1), (0, -1), (1, 1), (1, -1), (-1, 1), (-1, -1)]
    slabs = [moved(slab, *way) for slab, way in zip(slabs, ways)]
    group = divisor(planes, 6)
    u_new, velocity = pl.pallas_call(
        functools.partial(read_kernel, size_x, size_y, time_step),
        out_shape=[
            jax.ShapeDtypeStruct(u_old.shape, f32),
            jax.ShapeDtypeStruct((3, markers), f32),
        ],
        in_specs=[whole] * 17,
        out_specs=[whole] * 2,
        scratch_shapes=[
            pltpu.VMEM((3, planes, rows, depth), f32),
            pltpu.VMEM((lines, markers), f32),
            pltpu.VMEM((rows, markers), f32),
            pltpu.VMEM((3 * depth, markers), bf16),
            pltpu.VMEM((planes // group, group * 3 * rows, 3 * depth), bf16),
        ],
        compiler_params=params,
        cost_estimate=cost,
        name="read",
    )(feat, base, grid, u_old, density, low_x, high_x, low_y, high_y, *slabs)
    return (u_new, velocity.reshape(3, slots, width))


def solution(mesh):
    in_specs = (
        P(None, "gx", "gy", None),
        P("gx", "gy", None),
        P(None, ("gx", "gy"), None),
        P(None, ("gx", "gy"), None),
        P(("gx", "gy"), None),
        P(("gx", "gy"), None),
        P(("gx", "gy"), None),
        P(("gx", "gy")),
    )
    out_specs = (P(None, "gx", "gy", None), P(None, ("gx", "gy"), None))
    return jax.shard_map(
        on_device, mesh=mesh, in_specs=in_specs, out_specs=out_specs, check_vma=False
    )
```

time: 209 us -> 107 us (0.51)
  matrix products: 69.3 us -> 0 us
  Pallas kernels: 0 us -> 47.3 us
  local copies, waits for them, and re-layouts: 54.2 us -> 11.3 us
  other arithmetic: 42.5 us -> 3.14 us
  starting transfers between devices: 11.6 us -> 19 us
  waiting for transfers between devices: 27.9 us -> 23.7 us
    dot_general x4 -> x0, matrix products: 69.3 us -> none  [the longest x2 36.5 us: read_block(): jnp.dot(plane, table, precision=lax.Precision.HIGHEST, preferred_element_...]
    pallas_call x0 -> x2, Pallas kernels: none -> 47.3 us  [the longest x1 25.5 us: on_device(): pl.pallas_call(functools.partial(read_kernel, size_x, size_y, time_step),...]
    mul x4 -> x0, local copies, waits for them, and re-layouts: 25.4 us -> none  [block_weights(): along_x[:, :, None] * along_y[:, None, :]]
    mul x8 -> x0, other arithmetic: 15.4 us -> none  [the longest x4 13.1 us: block_weights(): along_x[:, :, None] * along_y[:, None, :]]
    reshape x2 -> x0, local copies, waits for them, and re-layouts: 14 us -> none  [the longest x1 7.49 us: on_device(): grid = flat_grid.reshape(outer_x, outer_y, 3, depth_z).transpose(2, 0, 1, 3)]
    slice x4 -> x0, other arithmetic: 11.8 us -> none  [the longest x1 8.11 us: on_device(): u_pad = state_pad[:3] + time_step * grid / state_pad[3][None]]
    ppermute x8 -> x12, starting transfers between devices: 11.6 us -> 19 us  [the longest x4 8.94 us: moved(): return lax.ppermute(value, ('gx', 'gy'), pairs)]
    add x17 -> x0, other arithmetic: 5.85 us -> none  [the longest x1 2.33 us: on_device(): u_pad = state_pad[:3] + time_step * grid / state_pad[3][None]]
  transfers between devices with their start and end apart: 8 -> 12, of which waited for: 7 -> 3; matrix products, arithmetic and copies ran while one was open for 12% -> 10% of each run, Pallas kernels for 0% -> 21%
where the time goes in v1:
time: 107 us; the launch traced here: 106 us
  Pallas kernels  47.3 us (44%)
  waiting for transfers between devices  23.7 us (22%)
  starting transfers between devices  19 us (18%)
  local copies, waits for them, and re-layouts  11.3 us (11%)
  other arithmetic  3.14 us (3%)
  between operations  1.55 us (1%)
    pallas_call x1, Pallas kernels, on_device(): pl.pallas_call(functools.partial(read_kernel, size_x, size_y, time_step),...  25.5 us
    ppermute x4, waiting for transfers between devices, moved(): return lax.ppermute(value, 'gy', [(i, (i + step_y) % n) for i in range(n)])  23.6 us
    pallas_call x1, Pallas kernels, on_device(): pl.pallas_call(functools.partial(spread_kernel, size_x, size_y), out_shap...  21.8 us
    ppermute x4, starting transfers between devices, moved(): return lax.ppermute(value, ('gx', 'gy'), pairs)  8.94 us
    ppermute x4, starting transfers between devices, moved(): return lax.ppermute(value, 'gx', [(i, (i + step_x) % n) for i in range(n)])  6.18 us
    ppermute x4, starting transfers between devices, moved(): return lax.ppermute(value, 'gy', [(i, (i + step_y) % n) for i in range(n)])  3.93 us
    slice x2, local copies, waits for them, and re-layouts, strip(): inner = jnp.concatenate([u_old[:, :, r], density[None, :, r]], axis=0)  3.03 us
    unnamed x31, local copies, waits for them, and re-layouts  2.48 us
  transfers between devices with their start and end apart: 12, of which 3 were waited for; matrix products, arithmetic and copies ran while one was open for 10% of the time, Pallas kernels for 21%

profile of v1, /device:TPU:0, one launch (start us, length us, event | category | flops | bytes accessed | tf_op | source)
XLA Modules:
  0.0 106.1 jit_solution(14528928824812117126)
XLA Ops:
  0.6 0.8 slice.49
  1.4 0.9 slice.48
  3.1 0.8 slice.51
  4.0 0.9 slice.50
  5.3 2.9 %collective-permute-start.1 = (f32[4,2,32,256]{3,1,0,2:T(2,128)S(1)}, f32[4,2,32,256]{3,1,0,2:T(2,128)S(1)}, u32[]{:S(2)}, u32[]{:S(2)}) collective-permute-start(f32[4,2,32,256]{3,1,0,2:T(2,128)S(1)} %pad_maximum_fusion.1), channel_id=1, source_target_pairs={{0,28},{4,0},{8,4},{12,8},{16,12},{20,16},{24,20},{28,24},{1,29},{... | collective-permute-start | bytes 786440 | tf_op jit(solution)/shard_map/ppermute | solution.py:20
  8.9 0.8 multiply_bitcast_fusion
  9.7 0.8 copy_bitcast_fusion.4
  10.4 1.4 %pad_add_fusion.base.refs_1_ = s32[3,2048]{1,0:T(4,128)} fusion(s32[1,2048]{1,0:T(1,128)} %bitcast.71, s32[1,2048]{1,0:T(1,128)} %bitcast.72, s32[1,2048]{1,0:T(1,128)} %bitcast.73), kind=kLoop, calls=%fused_computation.13 | loop fusion | flops 12288 | bytes 49152 | tf_op jit(solution)/shard_map/stack | solution.py:213
  12.5 21.8 %spread.1 = (f32[3,35,40,256]{3,2,1,0:T(8,128)}, f32[3,3,40,256]{3,2,1,0:T(8,128)}, f32[3,3,40,256]{3,2,1,0:T(8,128)}, f32[3,3,35,256]{3,2,1,0:T(8,128)}, f32[3,...) custom-call(f32[7,2048]{1,0:T(8,128)} %pad_maximum_fusion.3.feat.ref, ...), custom_call_target="tpu_custom_call" | custom-call | flops 13212057600 | bytes 2867200 | tf_op jit(solution)/shard_map/spread/pallas_call | solution.py:233
  34.3 0.9 collective-permute-start.8
  35.2 3.4 %collective-permute-start.9 = (f32[3,3,3,256]{3,2,1,0:T(4,128)}, f32[3,3,3,256]{3,2,1,0:T(4,128)S(1)}, u32[]{:S(2)}, u32[]{:S(2)}) collective-permute-start(f32[3,3,3,256]{3,2,1,0:T(4,128)} %get-tuple-element.19), channel_id=1, source_target_pairs={{0,7},{1,4},{2,5},{3,6},{4,11},{5,8},{6,9},{7,10},{8,15},{9,12},{1... | collective-permute-start | bytes 82952 | tf_op jit(solution)/shard_map/ppermute | solution.py:30
  38.6 1.1 %collective-permute-start.10 = (f32[3,3,3,256]{3,2,1,0:T(4,128)}, f32[3,3,3,256]{3,2,1,0:T(4,128)S(1)}, u32[]{:S(2)}, u32[]{:S(2)}) collective-permute-start(f32[3,3,3,256]{3,2,1,0:T(4,128)} %get-tuple-element.20), channel_id=1, source_target_pairs={{0,29},{1,30},{2,31},{3,28},{4,1},{5,2},{6,3},{7,0},{8,5},{9,6},{1... | collective-permute-start | bytes 82952 | tf_op jit(solution)/shard_map/ppermute | solution.py:30
  39.7 1.8 %fusion = (f32[3,32,1,256]{3,2,1,0:T(1,128)S(1)}, f32[3,32,1,256]{3,2,1,0:T(1,128)S(1)}, f32[3,32,1,256]{3,2,1,0:T(1,128)S(1)}) fusion(f32[3,32,32,256]{3,2,1,0:T(8,128)} %refs_3_.1), kind=kLoop, calls=%fused_computation.27 | loop fusion | bytes 589824 | tf_op jit(solution)/shard_map/slice | solution.py:220
  41.6 1.2 %fusion.1 = (f32[32,1,256]{2,1,0:T(1,128)S(1)}, f32[32,1,256]{2,1,0:T(1,128)S(1)}, f32[32,1,256]{2,1,0:T(1,128)S(1)}) fusion(f32[32,32,256]{2,1,0:T(8,128)} %refs_4_.1), kind=kLoop, calls=%fused_computation.28 | loop fusion | bytes 196608 | tf_op jit(solution)/shard_map/slice | solution.py:220
  42.8 3.5 %collective-permute-start.11 = (f32[3,3,3,256]{3,2,1,0:T(4,128)}, f32[3,3,3,256]{3,2,1,0:T(4,128)S(1)}, u32[]{:S(2)}, u32[]{:S(2)}) collective-permute-start(f32[3,3,3,256]{3,2,1,0:T(4,128)} %get-tuple-element.21), channel_id=1, source_target_pairs={{0,31},{1,28},{2,29},{3,30},{4,3},{5,0},{6,1},{7,2},{8,7},{9,4},{1... | collective-permute-start | bytes 82952 | tf_op jit(solution)/shard_map/ppermute | solution.py:30
  46.5 1.0 collective-permute-start.4
  47.5 1.7 %collective-permute-start.5 = (f32[3,3,40,256]{3,2,1,0:T(8,128)}, f32[3,3,40,256]{3,2,1,0:T(8,128)S(1)}, u32[]{:S(2)}, u32[]{:S(2)}) collective-permute-start(f32[3,3,40,256]{3,2,1,0:T(8,128)} %get-tuple-element.15), channel_id=1, source_target_pairs={{0,28},{4,0},{8,4},{12,8},{16,12},{20,16},{24,20},{28,24},{1,29},{... | collective-permute-start | bytes 1105928 | tf_op jit(solution)/shard_map/ppermute | solution.py:20
  49.2 3.8 %collective-permute-start.7 = (f32[3,3,35,256]{3,2,1,0:T(8,128)}, f32[3,3,35,256]{3,2,1,0:T(8,128)S(1)}, u32[]{:S(2)}, u32[]{:S(2)}) collective-permute-start(f32[3,3,35,256]{3,2,1,0:T(8,128)} %get-tuple-element.17), channel_id=1, source_target_pairs={{0,3},{1,0},{2,1},{3,2},{4,7},{5,4},{6,5},{7,6},{8,11},{9,8},{10,9... | collective-permute-start | bytes 967688 | tf_op jit(solution)/shard_map/ppermute | solution.py:23
  53.2 6.8 %collective-permute-done.6.refs_11_ = f32[3,3,35,256]{3,2,1,0:T(8,128)S(1)} collective-permute-done((f32[3,3,35,256]{3,2,1,0:T(8,128)}, f32[3,3,35,256]{3,2,1,0:T(8,128)S(1)}, u32[]{:S(2)}, u32[]{:S(2)}) %collective-permute-start.6) | collective-permute-done | bytes 322592 | tf_op jit(solution)/shard_map/ppermute | solution.py:23
  60.7 0.8 copy.21.refs_6_
  61.5 6.4 %collective-permute-done.7.refs_12_ = f32[3,3,35,256]{3,2,1,0:T(8,128)S(1)} collective-permute-done((f32[3,3,35,256]{3,2,1,0:T(8,128)}, f32[3,3,35,256]{3,2,1,0:T(8,128)S(1)}, u32[]{:S(2)}, u32[]{:S(2)}) %collective-permute-start.7) | collective-permute-done | bytes 322592 | tf_op jit(solution)/shard_map/ppermute | solution.py:23
  67.9 10.5 %collective-permute-done.2.refs_7_ = f32[4,1,35,256]{3,2,1,0:T(8,128)S(1)} collective-permute-done((f32[4,1,35,256]{3,2,1,0:T(8,128)S(1)}, f32[4,1,35,256]{3,2,1,0:T(8,128)S(1)}, u32[]{:S(2)}, u32[]{:S(2)}) %collective-permute-start.2) | collective-permute-done | bytes 143392 | tf_op jit(solution)/shard_map/ppermute | solution.py:23
  79.1 25.5 %read.1 = (f32[3,32,32,256]{3,2,1,0:T(8,128)}, f32[3,2048]{1,0:T(4,128)}) custom-call(f32[7,2048]{1,0:T(8,128)} %pad_maximum_fusion.3.feat.refs_0_, s32[3,2048]{1,0:T(4,128)} %pad_add_fusion.base.refs_1_, f32[3,35,40,256]{3,2,1,0:T(8,128)} %get-tuple-element.13.refs_2_, f32[3,32,32,256]{3,2,1,0:T(8,128)} %refs_3_.1, f32[32,32,256]{2,1,0:T(8,128)} %refs_4_.1, ...), custom_call_target="tpu_custom_call" | custom-call | flops 13212057600 | bytes 2867200 | tf_op jit(solution)/shard_map/read/pallas_call | solution.py:254
  104.7 1.4 %copy.54 = f32[1,3,16,128]{3,2,1,0:T(8,128)} copy(f32[1,3,16,128]{3,1,2,0:T(4,128)} %bitcast.67) | data formatting | bytes 49152
  (54 shorter events, 3.6 us)
Async XLA Ops:
  2.6 40.2 %collective-permute-start = (f32[4,1,32,256]{3,1,2,0:T(1,128)S(1)}, f32[4,1,32,256]{3,1,2,0:T(1,128)S(1)}, u32[]{:S(2)}, u32[]{:S(2)}) collective-permute-start(f32[4,1,32,256]{3,1,2,0:T(1,128)S(1)} %pad_maximum_fusion.2), channel_id=1, source_target_pairs={{0,4},{4,8},{8,12},{12,16},{16,20},{20,24},{24,28},{28,0},{1,5},{5... | collective-permute-start | bytes 393224 | tf_op jit(solution)/shard_map/ppermute | solution.py:20
  5.3 41.1 %collective-permute-start.1 = (f32[4,2,32,256]{3,1,0,2:T(2,128)S(1)}, f32[4,2,32,256]{3,1,0,2:T(2,128)S(1)}, u32[]{:S(2)}, u32[]{:S(2)}) collective-permute-start(f32[4,2,32,256]{3,1,0,2:T(2,128)S(1)} %pad_maximum_fusion.1), channel_id=1, source_target_pairs={{0,28},{4,0},{8,4},{12,8},{16,12},{20,16},{24,20},{28,24},{1,29},{... | collective-permute-start | bytes 786440 | tf_op jit(solution)/shard_map/ppermute | solution.py:20
  34.3 12.2 %collective-permute-start.8 = (f32[3,3,3,256]{3,2,1,0:T(4,128)}, f32[3,3,3,256]{3,2,1,0:T(4,128)S(1)}, u32[]{:S(2)}, u32[]{:S(2)}) collective-permute-start(f32[3,3,3,256]{3,2,1,0:T(4,128)} %get-tuple-element.18), channel_id=1, source_target_pairs={{0,5},{1,6},{2,7},{3,4},{4,9},{5,10},{6,11},{7,8},{8,13},{9,14},{1... | collective-permute-start | bytes 82952 | tf_op jit(solution)/shard_map/ppermute | solution.py:30
  35.2 12.3 %collective-permute-start.9 = (f32[3,3,3,256]{3,2,1,0:T(4,128)}, f32[3,3,3,256]{3,2,1,0:T(4,128)S(1)}, u32[]{:S(2)}, u32[]{:S(2)}) collective-permute-start(f32[3,3,3,256]{3,2,1,0:T(4,128)} %get-tuple-element.19), channel_id=1, source_target_pairs={{0,7},{1,4},{2,5},{3,6},{4,11},{5,8},{6,9},{7,10},{8,15},{9,12},{1... | collective-permute-start | bytes 82952 | tf_op jit(solution)/shard_map/ppermute | solution.py:30
  38.6 10.6 %collective-permute-start.10 = (f32[3,3,3,256]{3,2,1,0:T(4,128)}, f32[3,3,3,256]{3,2,1,0:T(4,128)S(1)}, u32[]{:S(2)}, u32[]{:S(2)}) collective-permute-start(f32[3,3,3,256]{3,2,1,0:T(4,128)} %get-tuple-element.20), channel_id=1, source_target_pairs={{0,29},{1,30},{2,31},{3,28},{4,1},{5,2},{6,3},{7,0},{8,5},{9,6},{1... | collective-permute-start | bytes 82952 | tf_op jit(solution)/shard_map/ppermute | solution.py:30
  42.8 10.2 %collective-permute-start.11 = (f32[3,3,3,256]{3,2,1,0:T(4,128)}, f32[3,3,3,256]{3,2,1,0:T(4,128)S(1)}, u32[]{:S(2)}, u32[]{:S(2)}) collective-permute-start(f32[3,3,3,256]{3,2,1,0:T(4,128)} %get-tuple-element.21), channel_id=1, source_target_pairs={{0,31},{1,28},{2,29},{3,30},{4,3},{5,0},{6,1},{7,2},{8,7},{9,4},{1... | collective-permute-start | bytes 82952 | tf_op jit(solution)/shard_map/ppermute | solution.py:30
  46.4 13.6 %collective-permute-start.6 = (f32[3,3,35,256]{3,2,1,0:T(8,128)}, f32[3,3,35,256]{3,2,1,0:T(8,128)S(1)}, u32[]{:S(2)}, u32[]{:S(2)}) collective-permute-start(f32[3,3,35,256]{3,2,1,0:T(8,128)} %get-tuple-element.16), channel_id=1, source_target_pairs={{0,1},{1,2},{2,3},{3,0},{4,5},{5,6},{6,7},{7,4},{8,9},{9,10},{10,1... | collective-permute-start | bytes 967688 | tf_op jit(solution)/shard_map/ppermute | solution.py:23
  46.5 31.9 %copy-start.6 = (f32[3,3,3,256]{3,2,1,0:T(4,128)}, f32[3,3,3,256]{3,2,1,0:T(4,128)S(1)}, u32[]{:S(2)}) copy-start(f32[3,3,3,256]{3,2,1,0:T(4,128)S(1)} %collective-permute-done.8.refs_13_) | copy-start | bytes 82948
  46.5 21.4 %collective-permute-start.4 = (f32[3,3,40,256]{3,2,1,0:T(8,128)}, f32[3,3,40,256]{3,2,1,0:T(8,128)S(1)}, u32[]{:S(2)}, u32[]{:S(2)}) collective-permute-start(f32[3,3,40,256]{3,2,1,0:T(8,128)} %get-tuple-element.14), channel_id=1, source_target_pairs={{0,4},{4,8},{8,12},{12,16},{16,20},{20,24},{24,28},{28,0},{1,5},{5... | collective-permute-start | bytes 1105928 | tf_op jit(solution)/shard_map/ppermute | solution.py:20
  47.5 30.8 %copy-start.7 = (f32[3,3,3,256]{3,2,1,0:T(4,128)}, f32[3,3,3,256]{3,2,1,0:T(4,128)S(1)}, u32[]{:S(2)}) copy-start(f32[3,3,3,256]{3,2,1,0:T(4,128)S(1)} %collective-permute-done.9.refs_14_) | copy-start | bytes 82948
  47.5 20.4 %collective-permute-start.5 = (f32[3,3,40,256]{3,2,1,0:T(8,128)}, f32[3,3,40,256]{3,2,1,0:T(8,128)S(1)}, u32[]{:S(2)}, u32[]{:S(2)}) collective-permute-start(f32[3,3,40,256]{3,2,1,0:T(8,128)} %get-tuple-element.15), channel_id=1, source_target_pairs={{0,28},{4,0},{8,4},{12,8},{16,12},{20,16},{24,20},{28,24},{1,29},{... | collective-permute-start | bytes 1105928 | tf_op jit(solution)/shard_map/ppermute | solution.py:20
  49.2 29.2 %copy-start.8 = (f32[3,3,3,256]{3,2,1,0:T(4,128)}, f32[3,3,3,256]{3,2,1,0:T(4,128)S(1)}, u32[]{:S(2)}) copy-start(f32[3,3,3,256]{3,2,1,0:T(4,128)S(1)} %collective-permute-done.10.refs_15_) | copy-start | bytes 82948
  49.2 18.7 %collective-permute-start.7 = (f32[3,3,35,256]{3,2,1,0:T(8,128)}, f32[3,3,35,256]{3,2,1,0:T(8,128)S(1)}, u32[]{:S(2)}, u32[]{:S(2)}) collective-permute-start(f32[3,3,35,256]{3,2,1,0:T(8,128)} %get-tuple-element.17), channel_id=1, source_target_pairs={{0,3},{1,0},{2,1},{3,2},{4,7},{5,4},{6,5},{7,6},{8,11},{9,8},{10,9... | collective-permute-start | bytes 967688 | tf_op jit(solution)/shard_map/ppermute | solution.py:23
  53.0 25.3 %copy-start.9 = (f32[3,3,3,256]{3,2,1,0:T(4,128)}, f32[3,3,3,256]{3,2,1,0:T(4,128)S(1)}, u32[]{:S(2)}) copy-start(f32[3,3,3,256]{3,2,1,0:T(4,128)S(1)} %collective-permute-done.11.refs_16_) | copy-start | bytes 82948
  53.1 25.3 %collective-permute-start.3 = (f32[4,2,35,256]{3,2,1,0:T(8,128)S(1)}, f32[4,2,35,256]{3,2,1,0:T(8,128)S(1)}, u32[]{:S(2)}, u32[]{:S(2)}) collective-permute-start(f32[4,2,35,256]{3,2,1,0:T(8,128)S(1)} %pad_maximum_fusion), channel_id=1, source_target_pairs={{0,3},{1,0},{2,1},{3,2},{4,7},{5,4},{6,5},{7,6},{8,11},{9,8},{10,9... | collective-permute-start | bytes 860168 | tf_op jit(solution)/shard_map/ppermute | solution.py:23
  60.0 18.4 %copy-start = (f32[3,3,35,256]{3,2,1,0:T(8,128)}, f32[3,3,35,256]{3,2,1,0:T(8,128)S(1)}, u32[]{:S(2)}) copy-start(f32[3,3,35,256]{3,2,1,0:T(8,128)S(1)} %collective-permute-done.6.refs_11_) | copy-start | bytes 967684
  60.0 18.4 %collective-permute-start.2 = (f32[4,1,35,256]{3,2,1,0:T(8,128)S(1)}, f32[4,1,35,256]{3,2,1,0:T(8,128)S(1)}, u32[]{:S(2)}, u32[]{:S(2)}) collective-permute-start(f32[4,1,35,256]{3,2,1,0:T(8,128)S(1)} %maximum_bitcast_fusion), channel_id=1, source_target_pairs={{0,1},{1,2},{2,3},{3,0},{4,5},{5,6},{6,7},{7,4},{8,9},{9,10},{10,1... | collective-permute-start | bytes 430088 | tf_op jit(solution)/shard_map/ppermute | solution.py:23
  67.9 10.5 %copy-start.3 = (f32[3,3,35,256]{3,2,1,0:T(8,128)}, f32[3,3,35,256]{3,2,1,0:T(8,128)S(1)}, u32[]{:S(2)}) copy-start(f32[3,3,35,256]{3,2,1,0:T(8,128)S(1)} %collective-permute-done.7.refs_12_) | copy-start | bytes 967684
  67.9 10.5 %copy-start.1 = (f32[3,3,40,256]{3,2,1,0:T(8,128)}, f32[3,3,40,256]{3,2,1,0:T(8,128)S(1)}, u32[]{:S(2)}) copy-start(f32[3,3,40,256]{3,2,1,0:T(8,128)S(1)} %collective-permute-done.4.refs_9_) | copy-start | bytes 1105924
  67.9 10.5 %copy-start.2 = (f32[3,3,40,256]{3,2,1,0:T(8,128)}, f32[3,3,40,256]{3,2,1,0:T(8,128)S(1)}, u32[]{:S(2)}) copy-start(f32[3,3,40,256]{3,2,1,0:T(8,128)S(1)} %collective-permute-done.5.refs_10_) | copy-start | bytes 1105924
  78.4 0.7 copy-start.5
  78.4 0.8 copy-start.4
